TPU v7x, 32 devices: a whole 2x2x4 slice. The times are simulated.
32 devices in a mesh: days: 4 (over y, x), space: 8 (over z, core).
Axes of the slice: x: 2, y: 2, z: 4, core: 2. Of those that a mesh axis runs over, the one named last changes fastest.
Arguments:
- fields: bfloat16 [640, 32, 1440], P('days', 'space')
- month_label: int32 [640], P('days'), may hold values from 0 to 11, as said below
- row_index: int32 [32], P('space'), may hold values from 0 to 31
- area_table: float32 [32], replicated, may hold values from 0.05 to 1
- basis: bfloat16 [64, 32, 1440], P(None, 'space'), may hold values from -6 to 6
Outputs:
- eofs: float32 [64, 32, 1440], P(None, 'space')
- pcs: float32 [640, 64], P('days')
Inputs may be any that keep to these rules, and one draw needn't show every extreme that they name: `month_label`: each day's label differs from floor(12 * day / 640) by at most one; the first day with a given value of floor(12 * day / 640) carries exactly that value; every month labels at least one day.
All inputs are finite; a program needn't handle non-finite values.
Results may differ from a plain program's by a relative error of at most 0.0003.
Values sent between devices are 32-bit elements; how exact they have to be, the bound alone decides.
A program may use at most 64 MiB of HBM per device.

v0:
```python
import functools

import jax
import jax.numpy as jnp
from jax import lax
from jax.experimental import pallas as pl
from jax.experimental.pallas import tpu as pltpu
from jax.sharding import PartitionSpec as P

ITERS = 2
MESH = pl.DeviceIdType.MESH
HIGH = lax.Precision.HIGHEST
F32 = jnp.float32
BF16 = jnp.bfloat16
LANES = 128


def up(value, step):
    return -(-value // step) * step


def nt(a, b, **kw):
    return lax.dot_general(a, b, (((1,), (1,)), ((), ())), preferred_element_type=F32, **kw)


def nn(a, b, **kw):
    return lax.dot_general(a, b, (((1,), (0,)), ((), ())), preferred_element_type=F32, **kw)


def split3(x):
    high = x.astype(BF16)
    rest = x - high.astype(F32)
    mid = rest.astype(BF16)
    low = (rest - mid.astype(F32)).astype(BF16)
    return jnp.concatenate([high, mid, low], axis=0)


def join3(x, n):
    return x[:n] + (x[n : 2 * n] + x[2 * n :])


def inverse_factor(gram):
    n = gram.shape[0]
    sub = lax.broadcasted_iota(jnp.int32, (n, 1), 0)
    eye = (lax.broadcasted_iota(jnp.int32, (n, n), 0) == lax.broadcasted_iota(jnp.int32, (n, n), 1)).astype(F32)
    work = jnp.concatenate([gram, eye], axis=1)
    for j in range(n):
        row = work[j : j + 1, :]
        column = work[:, j : j + 1]
        inv = lax.rsqrt(work[j : j + 1, j : j + 1])
        row = row * inv
        work = jnp.where(sub == j, row, work - jnp.where(sub > j, column * inv, 0.0) * row)
    return work[:, n:]


def kernel(nd, ns, days_total, f_ref, b_ref, i_ref, a_ref, l_ref, eofs_ref, pcs_ref,
           send_f, recv_f, full_f, p_part, p_rs, p_mine, p_all, q_all,
           x_out, x_rs, x_day, x_all, c_all, tall, s_ref,
           sem_f, sem_prs, sem_pag, sem_pd, sem_xrs, sem_xd, sem_xag, sem_c):
    lat, dl, lon = f_ref.shape
    modes = eofs_ref.shape[0]
    rows = lat // nd
    day, space = lax.axis_index("days"), lax.axis_index("space")

    def peer(me, k, n):
        if n & (n - 1):
            return lax.rem(me + k, n), lax.rem(me + n - k, n)
        other = me
        for bit in range(n.bit_length()):
            if (k >> bit) & 1:
                other = other + (1 << bit) * (1 - 2 * lax.rem(lax.div(me, 1 << bit), 2))
        return other, other

    def copy(src, dst, sems, index, axis, target):
        return pltpu.make_async_remote_copy(
            src_ref=src, dst_ref=dst, send_sem=sems.at[(0,) + index], recv_sem=sems.at[(1,) + index],
            device_id={axis: target}, device_id_type=MESH)

    barrier = pltpu.get_barrier_semaphore()
    for k in range(1, nd):
        pl.semaphore_signal(barrier, inc=1, device_id={"days": peer(day, k, nd)[0]}, device_id_type=MESH)
    for k in range(1, ns):
        pl.semaphore_signal(barrier, inc=1, device_id={"space": peer(space, k, ns)[0]}, device_id_type=MESH)
    pl.semaphore_wait(barrier, nd + ns - 2)

    f_sent = []

    def send_fields(k):
        to = peer(day, k, nd)[0]
        for r in range(rows):
            send_f[k - 1, r] = f_ref[to * rows + r].astype(F32)
        c = copy(send_f.at[k - 1], recv_f.at[day], sem_f, (k - 1,), "days", to)
        c.start()
        f_sent.append(c)

    for k in range(1, nd - 1):
        send_fields(k)
    scales = [jnp.sqrt(jnp.full((1, 1), a_ref[i_ref[l]], F32)) for l in range(lat)]
    for l in range(lat):
        s_ref[l] = scales[l]

    total = None
    for l in range(lat):
        term = nt(f_ref[l], b_ref[:, l, :]) * scales[l]
        total = term if total is None else total + term
    height, wide = p_part.shape[1:]
    total = jnp.concatenate([total, jnp.zeros((dl, wide - modes), F32)], axis=1)
    p_part[...] = jnp.zeros_like(p_part)
    for t in range(ns):
        have = min(dl, (t + 1) * height) - t * height
        if have > 0:
            p_part[t, :have] = total[t * height : t * height + have]
    sent = []
    for k in range(1, ns):
        to = peer(space, k, ns)[0]
        c = copy(p_part.at[to], p_rs.at[k - 1], sem_prs, (k - 1,), "space", to)
        c.start()
        sent.append(c)
    acc = p_part[space]
    for k in range(1, ns):
        sent[k - 1].wait()
        acc = acc + p_rs[k - 1]
    p_all[space] = acc
    sent = []
    for k in range(1, ns):
        to = peer(space, k, ns)[0]
        c = copy(p_all.at[space], p_all.at[space], sem_pag, (k - 1,), "space", to)
        c.start()
        sent.append(c)
    for k in range(1, ns):
        sent[k - 1].wait_send()
        frm = peer(space, k, ns)[1]
        copy(p_all.at[frm], p_all.at[frm], sem_pag, (k - 1,), "space", frm).wait_recv()
    group = up(modes, LANES // 2)
    hot = (l_ref[...] == lax.broadcasted_iota(jnp.int32, (wide, dl), 0) - group).astype(F32)
    p_mine[...] = jnp.concatenate([p_all[t] for t in range(ns)], axis=0)[:dl] + hot.T
    sent = []
    q_all[day] = p_mine[...]
    for k in range(1, nd):
        to = peer(day, k, nd)[0]
        c = copy(p_mine, q_all.at[day], sem_pd, (k - 1,), "days", to)
        c.start()
        sent.append(c)
    send_fields(nd - 1)
    for r in range(rows):
        full_f[r, pl.ds(pl.multiple_of(day * dl, 16), dl)] = f_ref[day * rows + r]
    for k in range(1, nd):
        sent[k - 1].wait_send()
        frm = peer(day, k, nd)[1]
        copy(p_mine, q_all.at[frm], sem_pd, (k - 1,), "days", frm).wait_recv()
    qt = jnp.concatenate([q_all[j] for j in range(nd)], axis=0).T
    start = qt[:modes]
    months = qt[LANES // 2 :] if modes <= LANES // 2 else qt[up(modes, LANES) :]
    mean_of = months / jnp.maximum(jnp.sum(months, axis=1, keepdims=True), 1.0)

    def center(x):
        return x - nn(nt(x, mean_of, precision=HIGH), months, precision=HIGH)

    pcs = center(start)
    for k in range(1, nd):
        f_sent[k - 1].wait_send()
        frm = peer(day, k, nd)[1]
        copy(send_f.at[k - 1], recv_f.at[frm], sem_f, (k - 1,), "days", frm).wait_recv()
        for r in range(rows):
            full_f[r, pl.ds(pl.multiple_of(frm * dl, 16), dl)] = recv_f[frm, r].astype(BF16)

    part = modes // ns
    n_days = nd * dl
    gram_at = up(n_days, LANES)
    for it in range(ITERS):
        last = it == ITERS - 1
        pcs3 = split3(pcs)
        gram, raw = None, None
        for r in range(rows):
            scale = s_ref[day * rows + r]
            cover = join3(nn(pcs3, full_f[r]), modes) * (scale * (1.0 / days_total))
            if last:
                c_all[day, r] = cover
            term = nt(cover, cover, precision=HIGH)
            gram = term if gram is None else gram + term
            term = join3(nt(split3(cover * scale), full_f[r]), modes)
            raw = term if raw is None else raw + term
        x_out[it, :, :n_days] = raw
        x_out[it, :, n_days:] = jnp.zeros((modes, x_out.shape[2] - n_days), F32)
        x_out[it, :, gram_at : gram_at + modes] = gram
        sent = []
        for k in range(1, ns):
            to = peer(space, k, ns)[0]
            c = copy(x_out.at[it, pl.ds(pl.multiple_of(to * part, part), part)], x_rs.at[it, k - 1],
                     sem_xrs, (it, k - 1), "space", to)
            c.start()
            sent.append(c)
        acc = x_out[it, pl.ds(pl.multiple_of(space * part, part), part)]
        for k in range(1, ns):
            sent[k - 1].wait()
            acc = acc + x_rs[it, k - 1]
        x_day[it, day] = acc
        sent = []
        for k in range(1, nd):
            to = peer(day, k, nd)[0]
            c = copy(x_day.at[it, day], x_day.at[it, day], sem_xd, (it, k - 1), "days", to)
            c.start()
            sent.append(c)
        c_sent = []
        if last:
            for k in range(1, nd):
                to = peer(day, k, nd)[0]
                c = copy(c_all.at[day], c_all.at[day], sem_c, (k - 1,), "days", to)
                c.start()
                c_sent.append(c)
        for k in range(1, nd):
            sent[k - 1].wait_send()
            frm = peer(day, k, nd)[1]
            copy(x_day.at[it, frm], x_day.at[it, frm], sem_xd, (it, k - 1), "days", frm).wait_recv()
        acc = x_day[it, 0]
        for j in range(1, nd):
            acc = acc + x_day[it, j]
        x_all[it, space] = acc
        sent = []
        for k in range(1, ns):
            to = peer(space, k, ns)[0]
            c = copy(x_all.at[it, space], x_all.at[it, space], sem_xag, (it, k - 1), "space", to)
            c.start()
            sent.append(c)
        for k in range(1, ns):
            sent[k - 1].wait_send()
            frm = peer(space, k, ns)[1]
            copy(x_all.at[it, frm], x_all.at[it, frm], sem_xag, (it, k - 1), "space", frm).wait_recv()
        whole = jnp.concatenate([x_all[it, t] for t in range(ns)], axis=0)
        inv = inverse_factor(whole[:, gram_at : gram_at + modes])
        raw = center(whole[:, :n_days])
        if not last:
            pcs = nn(inv, raw, precision=HIGH)
    tall[...] = raw.T
    mine = tall[pl.ds(pl.multiple_of(day * dl, 8), dl)]
    pcs_ref[...] = nt(inv, mine, precision=HIGH)
    for k in range(1, nd):
        c_sent[k - 1].wait_send()
        frm = peer(day, k, nd)[1]
        copy(c_all.at[frm], c_all.at[frm], sem_c, (k - 1,), "days", frm).wait_recv()
    for j in range(nd):
        for r in range(rows):
            eofs_ref[:, j * rows + r, :] = nn(inv, c_all[j, r], precision=HIGH)


def solution(mesh):
    nd, ns = mesh.shape["days"], mesh.shape["space"]

    def local(fields, month_label, row_index, area_table, basis):
        dl, lat, lon = fields.shape
        modes = basis.shape[0]
        rows = lat // nd
        part = modes // ns
        group = up(modes, LANES // 2)
        wide = up(group + 12, LANES)
        height = up(-(-dl // ns), 8)
        n_days = nd * dl
        span = up(n_days, LANES) + up(modes, LANES)
        f_t = jnp.transpose(fields, (1, 0, 2))
        v, dma = pltpu.VMEM, pltpu.SemaphoreType.DMA
        eofs, pcs = pl.pallas_call(
            functools.partial(kernel, nd, ns, n_days),
            out_shape=(jax.ShapeDtypeStruct((modes, lat, lon), F32), jax.ShapeDtypeStruct((modes, dl), F32)),
            in_specs=[pl.BlockSpec(memory_space=v)] * 2 + [pl.BlockSpec(memory_space=pltpu.SMEM)] * 2
            + [pl.BlockSpec(memory_space=v)],
            out_specs=(pl.BlockSpec(memory_space=v),) * 2,
            scratch_shapes=[
                v((nd - 1, rows, dl, lon), F32),
                v((nd, rows, dl, lon), F32),
                v((rows, n_days, lon), BF16),
                v((ns, height, wide), F32),
                v((ns - 1, height, wide), F32),
                v((dl, wide), F32),
                v((ns, height, wide), F32),
                v((nd, dl, wide), F32),
                v((ITERS, modes, span), F32),
                v((ITERS, ns - 1, part, span), F32),
                v((ITERS, nd, part, span), F32),
                v((ITERS, ns, part, span), F32),
                v((nd, rows, modes, lon), F32),
                v((n_days, modes), F32),
                v((lat, 1, 1), F32),
                dma((2, nd - 1)), dma((2, ns - 1)), dma((2, ns - 1)), dma((2, nd - 1)),
                dma((2, ITERS, ns - 1)), dma((2, ITERS, nd - 1)), dma((2, ITERS, ns - 1)), dma((2, nd - 1)),
            ],
            compiler_params=pltpu.CompilerParams(
                collective_id=0, has_side_effects=True, vmem_limit_bytes=60 * 1024 * 1024),
        )(f_t, basis, row_index, area_table, month_label[None, :])
        return eofs, pcs.T

    placed = (P("days", "space", None), P("days"), P("space"), P(), P(None, "space", None))
    return jax.shard_map(
        local,
        mesh=mesh,
        in_specs=placed,
        out_specs=(P(None, "space", None), P("days", None)),
        check_vma=False,
    )
```

profile of v0, /device:TPU:0, one launch (start us, length us, event | category | flops | bytes accessed | tf_op | source)
XLA Modules:
  0.0 115.1 jit_solution(360879041262705176)
XLA Ops:
  0.6 3.2 %copy.9 = bf16[160,4,1440]{2,0,1:T(8,128)(2,1)} copy(bf16[160,4,1440]{2,1,0:T(4,128)(2,1)} %param.5) | data formatting | bytes 3686400 | tf_op args[0]
  3.8 108.0 %shard_map.68 = (f32[64,4,1440]{2,1,0:T(4,128)}, f32[64,160]{1,0:T(8,128)}) custom-call(bf16[4,160,1440]{2,1,0:T(8,128)(2,1)} %bitcast.5, bf16[64,4,1440]{2,1,0:T(4,128)(2,1)} %b_ref.1, s32[4]{0:T(128)} %i_ref.1, f32[32]{0:T(128)} %a_ref.1, s32[1,160]{1,0:T(1,128)} %bitcast.7), custom_call_target="tpu_custom_call" | custom-call | tf_op jit(solution)/shard_map/pallas_call | solution.py:261
  111.8 0.0 copy-start
  111.8 2.7 %copy.12 = f32[64,4,1440]{2,1,0:T(4,128)} copy(f32[64,4,1440]{2,1,0:T(4,128)} %get-tuple-element.8) | data formatting | bytes 2949120
  114.5 0.0 copy-done
  114.5 0.6 copy.13
Async XLA Ops:
  111.8 2.7 %copy-start = (f32[64,160]{1,0:T(8,128)S(1)}, f32[64,160]{1,0:T(8,128)}, u32[]{:S(2)}) copy-start(f32[64,160]{1,0:T(8,128)} %get-tuple-element.5) | copy-start | bytes 122884
where the time goes:
time: 115 us
  Pallas kernels  108 us (94%)
  local copies, waits for them, and re-layouts  6.48 us (6%)
    pallas_call x1, Pallas kernels, local(): pl.pallas_call(functools.partial(kernel, nd, ns, n_days), out_shape=(jax....  108 us
    unnamed x5, local copies, waits for them, and re-layouts  6.48 us

commit v1 on v0

v1 whole, which is shorter than its diff:
```python
import functools

import jax
import jax.numpy as jnp
from jax import lax
from jax.experimental import pallas as pl
from jax.experimental.pallas import tpu as pltpu
from jax.sharding import PartitionSpec as P

ITERS = 2
MONTHS = 12
MESH = pl.DeviceIdType.MESH
HIGH = lax.Precision.HIGHEST
F32 = jnp.float32
BF16 = jnp.bfloat16
LANES = 128
CHUNK = 3 * LANES
EXTRA = 8
GRAM_AT = LANES // 2
BLOCK = 4


def nt(a, b, **kw):
    return lax.dot_general(a, b, (((1,), (1,)), ((), ())), preferred_element_type=F32, **kw)


def nn(a, b, **kw):
    return lax.dot_general(a, b, (((1,), (0,)), ((), ())), preferred_element_type=F32, **kw)


def split3(x):
    high = x.astype(BF16)
    rest = x - high.astype(F32)
    mid = rest.astype(BF16)
    low = (rest - mid.astype(F32)).astype(BF16)
    return jnp.concatenate([high, mid, low], axis=0)


def join3(x, n):
    return x[:n] + (x[n : 2 * n] + x[2 * n :])


def tree(terms):
    while len(terms) > 1:
        terms = [terms[i] + terms[i + 1] for i in range(0, len(terms), 2)]
    return terms[0]


def inverse_factor(tile):
    n = tile.shape[0]
    lane = lax.broadcasted_iota(jnp.int32, tile.shape, 1)
    sub = lax.broadcasted_iota(jnp.int32, tile.shape, 0)
    work = jnp.where(lane < GRAM_AT, (lane == sub).astype(F32), tile)
    for start in range(0, n, BLOCK):
        top = start // 8 * 8
        part = work[top:]
        rows = lax.broadcasted_iota(jnp.int32, part.shape, 0) + top
        at = GRAM_AT + start
        columns = [jnp.broadcast_to(part[:, at + t : at + t + 1], part.shape) for t in range(BLOCK)]
        for t in range(BLOCK):
            j = start + t
            k = j - top
            inv = lax.rsqrt(columns[t][k : k + 1])
            row = part[k : k + 1] * inv
            column = jnp.where(rows > j, columns[t] * inv, 0.0)
            for u in range(t + 1, BLOCK):
                columns[u] = columns[u] - column * column[k + u - t : k + u - t + 1]
            part = jnp.where(rows == j, row, part - column * row)
        work = part if top == 0 else jnp.concatenate([work[:top], part], axis=0)
    return work[:, :n]


def kernel(nd, ns, f_hbm, b_hbm, i_ref, a_ref, l_ref, eofs_ref, pcs_ref,
           f_in, b_in, own_f, send_f, recv_f, part_f, s_ref,
           u_out, r_one, v_out, r_two, blk, tl, c_send, c_recv, c_all,
           sem_l, sem_f, sem_one, sem_two, sem_b, sem_fw, sem_c, sem_g):
    dl, lat, lon = f_in.shape
    modes = eofs_ref.shape[0]
    hm = modes // 2
    base = dl // LANES * LANES
    tail = dl - base
    width = base + LANES
    nz = ns // 2
    chunks = [(at, min(CHUNK, lon - at)) for at in range(0, lon, CHUNK)]
    n_days = nd * dl
    day, space = lax.axis_index("days"), lax.axis_index("space")
    x, y = lax.rem(day, 2), lax.div(day, 2)
    c, z = lax.rem(space, 2), lax.div(space, 2)
    to_x, to_y, to_d = day + 1 - 2 * x, day + 2 - 4 * y, nd - 1 - day
    other = space + 1 - 2 * c
    row_of = (x, lat // 2 + y)
    row_out = (1 - x, lat // 2 + 1 - y)

    def flip(v, k):
        for bit in range(k.bit_length()):
            if (k >> bit) & 1:
                v = v + (1 << bit) * (1 - 2 * lax.rem(lax.div(v, 1 << bit), 2))
        return v

    def z_peer(k):
        return flip(z, k) * 2 + c

    started = []

    def describe(src, dst, sems, index, device):
        return pltpu.make_async_remote_copy(
            src_ref=src, dst_ref=dst, send_sem=sems.at[(0,) + index], recv_sem=sems.at[(1,) + index],
            device_id=device, device_id_type=MESH)

    def put(src, dst, sems, index, device):
        d = describe(src, dst, sems, index, device)
        d.start()
        started.append(d)

    def got(dst, sems, index, device):
        describe(dst, dst, sems, index, device).wait_recv()

    core = {"space": other}
    barrier = pltpu.get_barrier_semaphore()
    friends = [core] + [{"space": z_peer(k)} for k in range(1, nz)]
    for d in (to_x, to_y, to_d):
        friends += [{"days": d}, {"days": d, "space": other}]
    for friend in friends:
        pl.semaphore_signal(barrier, inc=1, device_id=friend, device_id_type=MESH)
    load_f = pltpu.make_async_copy(f_hbm, f_in, sem_l.at[0])
    load_b = pltpu.make_async_copy(b_hbm, b_in, sem_l.at[1])
    load_f.start()
    load_b.start()
    for l in range(lat):
        s_ref[l] = jnp.sqrt(jnp.full((1, 1), a_ref[i_ref[l]], F32))
    load_f.wait()
    for l in range(lat):
        own_f[l] = f_in[:, l, :]

    def fill(ab, i):
        at, w = chunks[i]
        send_f[ab, i, :, :w] = own_f[row_out[ab], :, at : at + w].astype(F32)

    def send_fields(i):
        w = chunks[i][1]
        for ab, to in ((0, to_x), (1, to_y)):
            put(send_f.at[ab, i], recv_f.at[ab, i], sem_f, (ab, i), {"days": to})

    early = len(chunks) - 1
    for i in range(len(chunks)):
        for ab in range(2):
            fill(ab, i)
        if i == 0:
            pl.semaphore_wait(barrier, len(friends))
        if i < early:
            send_fields(i)

    load_b.wait()
    total = None
    for l in range(lat):
        term = nt(b_in[:, l, :], own_f[l]) * s_ref[l]
        total = term if total is None else total + term

    lane = lax.broadcasted_iota(jnp.int32, (1, LANES), 1)

    def hot_of(labels):
        rows = lax.broadcasted_iota(jnp.int32, (LANES, dl), 0) - tail
        return (rows.astype(F32) == labels).astype(F32).astype(BF16)

    def reduce(st, hot):
        rows = hm + EXTRA if st == 0 else hm
        put(u_out.at[st, 0, 1 - c], r_one.at[st, 0], sem_one, (st, 0), core)
        if st > 0:
            for p, to in ((0, to_x), (1, to_y)):
                put(u_out.at[st, 1 + p, c], r_one.at[st, 1 + 2 * p], sem_one, (st, 1 + 2 * p), {"days": to})
                put(u_out.at[st, 1 + p, 1 - c], r_one.at[st, 2 + 2 * p], sem_one, (st, 2 + 2 * p), {"days": to, "space": other})
        return rows

    def finish(st, hot, last):
        rows = hm + EXTRA if st == 0 else hm
        mine = u_out[st, 0, c]
        got(r_one.at[st, 0], sem_one, (st, 0), core)
        near = r_one[st, 0]
        value = mine[:, :width] + near[:, :width]
        if st > 0:
            gram = (mine[:, base:width] + near[:, base:width], mine[:, width:] + near[:, width:])
            parts = []
            for p, to in ((0, to_x), (1, to_y)):
                got(r_one.at[st, 1 + 2 * p], sem_one, (st, 1 + 2 * p), {"days": to})
                got(r_one.at[st, 2 + 2 * p], sem_one, (st, 2 + 2 * p), {"days": to, "space": other})
                far = r_one[st, 1 + 2 * p, :, :width] + r_one[st, 2 + 2 * p, :, :width]
                value = value + far
                parts.append(gram[p] + far[:, base:])
            low = jnp.where(lane < GRAM_AT, value[:, base:], parts[0] + parts[1])
            v_out[st, :, :base] = value[:, :base]
            v_out[st, :, base:] = low
        else:
            v_out[st] = value
        for k in range(1, nz):
            put(v_out.at[st], r_two.at[st, k - 1], sem_two, (st, k - 1), {"space": z_peer(k)})
        for k in range(1, nz):
            got(r_two.at[st, k - 1], sem_two, (st, k - 1), {"space": z_peer(k)})
        value = tree([v_out[st]] + [r_two[st, k - 1] for k in range(1, nz)])
        month = join3(nt(split3(value[:, :dl]), hot), hm)
        blk[st, 0, c, :hm, :base] = value[:, :base]
        blk[st, 0, c, :hm, base:] = value[:, base:] + month
        if st == 0:
            names = jnp.broadcast_to(l_ref[...].astype(F32), (EXTRA, dl))
            blk[st, 0, c, hm:, :base] = names[:, :base]
            blk[st, 0, c, hm:, base:] = nt(jnp.ones((EXTRA, dl), BF16), hot)
            blk[st, 0, c, hm:, base:dl] = names[:, base:]
        mine = blk.at[st, 0, c, pl.ds(0, rows)]
        put(mine, mine, sem_b, (st, 3), core)
        for p, to in ((0, to_x), (1, to_y), (2, to_d)):
            if p < 2 and not last:
                put(mine, blk.at[st, 1 + p, c, pl.ds(0, rows)], sem_b, (st, p), {"days": to})
            else:
                put(blk.at[st, 0, c, pl.ds(0, rows), pl.ds(base, LANES)], tl.at[st, p, c, pl.ds(0, rows)], sem_b, (st, p), {"days": to})
        theirs = blk.at[st, 0, 1 - c, pl.ds(0, rows)]
        got(theirs, sem_b, (st, 3), core)

    def landed(st, last, p, half):
        rows = hm + EXTRA if st == 0 else hm
        if p < 2 and not last:
            return blk.at[st, 1 + p, half, pl.ds(0, rows)]
        return tl.at[st, p, half, pl.ds(0, rows)]

    def forward(st, last):
        for p, to in ((0, to_x), (1, to_y), (2, to_d)):
            ref = landed(st, last, p, c)
            got(ref, sem_b, (st, p), {"days": to})
            put(ref, ref, sem_fw, (st, p), core)
        for p in range(3):
            got(landed(st, last, p, 1 - c), sem_fw, (st, p), core)

    def both(st, b):
        return jnp.concatenate([blk[st, b, 0, :hm], blk[st, b, 1, :hm]], axis=0)

    def tiles(st, last):
        out = [both(st, 0)[:, base:]]
        for p in range(3):
            if p < 2 and not last:
                out.append(both(st, 1 + p)[:, base:])
            else:
                out.append(jnp.concatenate([tl[st, p, 0, :hm], tl[st, p, 1, :hm]], axis=0))
        return out

    def mean_of(st, last, scale):
        sums = tree(tiles(st, last))
        inside = (lane >= tail) & (lane < tail + MONTHS)
        return split3(jnp.where(inside, sums * scale, 0.0))

    def center(value, mean, hot):
        return value - join3(nn(mean, hot), modes)

    own_hot = hot_of(l_ref[...].astype(F32))
    for half in range(2):
        u_out[0, 0, half] = jnp.zeros((hm, width + LANES), F32)
        u_out[0, 0, half, :, :dl] = total[half * hm : (half + 1) * hm]
    reduce(0, own_hot)
    finish(0, own_hot, False)
    for i in range(early, len(chunks)):
        send_fields(i)
    forward(0, False)
    hots = [own_hot] + [hot_of(blk[0, 1 + p, 0, hm : hm + 1, :dl]) for p in range(2)]
    counts = tree([blk[0, b, 0, hm : hm + 1, base:] for b in range(3)] + [tl[0, 2, 0, hm : hm + 1]])
    per_day = 1.0 / jnp.maximum(counts, 1.0)
    mean = mean_of(0, False, per_day)
    patterns = [split3(center(both(0, b)[:, :dl], mean, hots[b])) for b in range(3)]

    for it in range(ITERS):
        st = it + 1
        last = it == ITERS - 1
        for i, (at, w) in enumerate(chunks):
            for ab, to, back in ((0, to_x, to_y), (1, to_y, to_x)):
                if it == 0:
                    got(recv_f.at[ab, i], sem_f, (ab, i), {"days": to})
                    part_f[ab, :, at : at + w] = recv_f[ab, i, :, :w].astype(BF16)
                cover = join3(nn(patterns[0], own_f[row_of[ab], :, at : at + w])
                              + nn(patterns[1 + ab], part_f[ab, :, at : at + w]), modes)
                c_send[it, ab, i, :, :w] = cover
                put(c_send.at[it, ab, i], c_recv.at[it, ab, i], sem_c, (it, ab, i), {"days": back})
        raw = [None] * 3
        gram = [None] * 2

        def add(sums, k, term):
            sums[k] = term if sums[k] is None else sums[k] + term

        def spread(i):
            w = chunks[i][1]
            for ab, to in ((0, to_x), (1, to_y)):
                ref = c_all.at[row_of[ab], i]
                put(ref, ref, sem_g, (ab, i), {"days": to})

        for i, (at, w) in enumerate(chunks):
            for ab, back in ((0, to_y), (1, to_x)):
                got(c_recv.at[it, ab, i], sem_c, (it, ab, i), {"days": back})
                scale = s_ref[row_of[ab]]
                cover = (c_send[it, ab, i, :, :w] + c_recv[it, ab, i, :, :w]) * (scale * (1.0 / n_days))
                if last:
                    c_all[row_of[ab], i, :, :w] = cover
                padded = jnp.concatenate([jnp.zeros((GRAM_AT, w), F32), cover], axis=0)
                add(gram, ab, nt(cover, padded, precision=HIGH))
                cover3 = split3(cover * scale)
                add(raw, 0, nt(cover3, own_f[row_of[ab], :, at : at + w]))
                add(raw, 1 + ab, nt(cover3, part_f[ab, :, at : at + w]))
            if last and i == 0:
                spread(0)
        for b in range(3):
            full = join3(raw[b], modes)
            for half in range(2):
                cut = slice(half * hm, (half + 1) * hm)
                u_out[st, b, half, :, base:width] = gram[max(b - 1, 0)][cut]
                if b == 0:
                    u_out[st, b, half, :, width:] = gram[1][cut]
                else:
                    u_out[st, b, half, :, width:] = jnp.zeros((hm, LANES), F32)
                u_out[st, b, half, :, :dl] = full[cut]
        reduce(st, own_hot)
        if last:
            for i in range(1, len(chunks)):
                spread(i)
        finish(st, own_hot, last)
        inv = inverse_factor(both(st, 0)[:, base:])
        if not last:
            forward(st, last)
            mean = mean_of(st, last, per_day)
            patterns = [split3(nn(inv, center(both(st, b)[:, :dl], mean, hots[b]), precision=HIGH)) for b in range(3)]
        else:
            for i, (at, w) in enumerate(chunks):
                for ab, to in ((0, to_x), (1, to_y)):
                    got(c_all.at[row_out[ab], i], sem_g, (ab, i), {"days": to})
                for l in range(lat):
                    eofs_ref[:, l, at : at + w] = nn(inv, c_all[l, i, :, :w], precision=HIGH)
            forward(st, last)
            mean = mean_of(st, last, per_day)
            pcs_ref[...] = nn(inv, center(both(st, 0)[:, :dl], mean, own_hot), precision=HIGH)
    for d in started:
        d.wait_send()


def solution(mesh):
    nd, ns = mesh.shape["days"], mesh.shape["space"]

    def local(fields, month_label, row_index, area_table, basis):
        dl, lat, lon = fields.shape
        modes = basis.shape[0]
        hm, nz = modes // 2, ns // 2
        base = dl // LANES * LANES
        width = base + LANES
        if nd != 4 or lat != nd or modes > GRAM_AT or dl - base + MONTHS > GRAM_AT or nz & (nz - 1):
            raise ValueError("unsupported sizes")
        n = -(-lon // CHUNK)
        stages = ITERS + 1
        v, dma = pltpu.VMEM, pltpu.SemaphoreType.DMA
        eofs, pcs = pl.pallas_call(
            functools.partial(kernel, nd, ns),
            out_shape=(jax.ShapeDtypeStruct((modes, lat, lon), F32), jax.ShapeDtypeStruct((modes, dl), F32)),
            in_specs=[pl.BlockSpec(memory_space=pl.ANY)] * 2 + [pl.BlockSpec(memory_space=pltpu.SMEM)] * 2
            + [pl.BlockSpec(memory_space=v)],
            out_specs=(pl.BlockSpec(memory_space=v),) * 2,
            scratch_shapes=[
                v((dl, lat, lon), BF16),
                v((modes, lat, lon), BF16),
                v((lat, dl, lon), BF16),
                v((2, n, dl, CHUNK), F32),
                v((2, n, dl, CHUNK), F32),
                v((2, dl, lon), BF16),
                v((lat, 1, 1), F32),
                v((stages, 3, 2, hm, width + LANES), F32),
                v((stages, 5, hm, width + LANES), F32),
                v((stages, hm, width), F32),
                v((stages, nz - 1, hm, width), F32),
                v((stages, 3, 2, hm + EXTRA, width), F32),
                v((stages, 3, 2, hm + EXTRA, LANES), F32),
                v((ITERS, 2, n, modes, CHUNK), F32),
                v((ITERS, 2, n, modes, CHUNK), F32),
                v((lat, n, modes, CHUNK), F32),
                dma((2,)), dma((2, 2, n)), dma((2, stages, 5)), dma((2, stages, nz - 1)),
                dma((2, stages, 4)), dma((2, stages, 3)), dma((2, ITERS, 2, n)), dma((2, 2, n)),
            ],
            compiler_params=pltpu.CompilerParams(
                collective_id=0, has_side_effects=True, vmem_limit_bytes=60 * 1024 * 1024),
        )(fields, basis, row_index, area_table, month_label[None, :])
        return eofs, pcs.T

    placed = (P("days", "space", None), P("days"), P("space"), P(), P(None, "space", None))
    return jax.shard_map(
        local,
        mesh=mesh,
        in_specs=placed,
        out_specs=(P(None, "space", None), P("days", None)),
        check_vma=False,
    )
```

time: 115 us -> 90.5 us (0.79)
  Pallas kernels: 108 us -> 86.3 us
  local copies, waits for them, and re-layouts: 6.48 us -> 3.32 us
    pallas_call x1, Pallas kernels: 108 us -> 86.3 us  [local(): pl.pallas_call(functools.partial(kernel, nd, ns), out_shape=(jax.ShapeDty...]
    unnamed x5 -> x4, local copies, waits for them, and re-layouts: 6.48 us -> 3.32 us
where the time goes in v1:
time: 90.5 us; the launch traced here: 90.3 us
  Pallas kernels  86.3 us (95%)
  local copies, waits for them, and re-layouts  3.32 us (4%)
    pallas_call x1, Pallas kernels, local(): pl.pallas_call(functools.partial(kernel, nd, ns), out_shape=(jax.ShapeDty...  86.3 us
    unnamed x4, local copies, waits for them, and re-layouts  3.32 us

profile of v1, /device:TPU:0, one launch (start us, length us, event | category | flops | bytes accessed | tf_op | source)
XLA Modules:
  0.0 90.3 jit_solution(11967479541073999270)
XLA Ops:
  0.6 86.3 %shard_map.68 = (f32[64,4,1440]{2,1,0:T(4,128)}, f32[64,160]{1,0:T(8,128)}) custom-call(bf16[160,4,1440]{2,1,0:T(4,128)(2,1)} %f_hbm.1, bf16[64,4,1440]{2,1,0:T(4,128)(2,1)} %b_hbm.1, s32[4]{0:T(128)} %i_ref.1, f32[32]{0:T(128)} %a_ref.1, s32[1,160]{1,0:T(1,128)} %bitcast.3), custom_call_target="tpu_custom_call" | custom-call | tf_op jit(solution)/shard_map/pallas_call | solution.py:351
  87.0 0.0 copy-start
  87.0 2.7 %copy.9 = f32[64,4,1440]{2,1,0:T(4,128)} copy(f32[64,4,1440]{2,1,0:T(4,128)} %get-tuple-element.8) | data formatting | bytes 2949120
  89.7 0.0 copy-done
  89.7 0.6 copy.10
Async XLA Ops:
  87.0 2.7 %copy-start = (f32[64,160]{1,0:T(8,128)S(1)}, f32[64,160]{1,0:T(8,128)}, u32[]{:S(2)}) copy-start(f32[64,160]{1,0:T(8,128)} %get-tuple-element.5) | copy-start | bytes 122884

commit v2 on v1

--- a/solution.py
+++ b/solution.py
@@ -44,6 +44,15 @@
     while len(terms) > 1:
         terms = [terms[i] + terms[i + 1] for i in range(0, len(terms), 2)]
     return terms[0]
+
+
+def pack(x, tail):
+    rows = x.shape[0] * tail // LANES
+    return jnp.concatenate([x[at : at + rows] for at in range(0, x.shape[0], rows)], axis=1)
+
+
+def unpack(x, tail):
+    return jnp.concatenate([x[:, at : at + tail] for at in range(0, LANES, tail)], axis=0)
 
 
 def inverse_factor(tile):
@@ -70,12 +79,19 @@
     return work[:, :n]
 
 
-def kernel(nd, ns, f_hbm, b_hbm, i_ref, a_ref, l_ref, eofs_ref, pcs_ref,
-           f_in, b_in, own_f, send_f, recv_f, part_f, s_ref,
-           u_out, r_one, v_out, r_two, blk, tl, c_send, c_recv, c_all,
-           sem_l, sem_f, sem_one, sem_two, sem_b, sem_fw, sem_c, sem_g):
+def last_kernel(inv_ref, cover_ref, pcs_ref, eofs_ref, out_ref):
+    inv = inv_ref[...]
+    for l in range(eofs_ref.shape[1]):
+        eofs_ref[:, l, :] = nn(inv, cover_ref[l, 0], precision=HIGH)
+    out_ref[...] = pcs_ref[...]
+
+
+def kernel(nd, ns, f_hbm, b_hbm, i_ref, a_ref, l_ref, cover_hbm, inv_ref, pcs_ref,
+           f_in, b_in, own_f, send_f, recv_f, send_t, recv_t, part_f, s_ref,
+           u_out, r_one, v_out, r_two, blk, tl, c_send, c_recv, c_all, t_send, t_recv, t_all,
+           sem_l, sem_f, sem_one, sem_two, sem_b, sem_fw, sem_c, sem_g, sem_o):
     dl, lat, lon = f_in.shape
-    modes = eofs_ref.shape[0]
+    modes = inv_ref.shape[0]
     hm = modes // 2
     base = dl // LANES * LANES
     tail = dl - base
@@ -83,6 +99,9 @@
     nz = ns // 2
     chunks = [(at, min(CHUNK, lon - at)) for at in range(0, lon, CHUNK)]
     n_days = nd * dl
+    rest = lon % LANES
+    final = len(chunks) - 1
+    full = [w // LANES * LANES for _, w in chunks]
     day, space = lax.axis_index("days"), lax.axis_index("space")
     x, y = lax.rem(day, 2), lax.div(day, 2)
     c, z = lax.rem(space, 2), lax.div(space, 2)
@@ -129,20 +148,39 @@
     for l in range(lat):
         s_ref[l] = jnp.sqrt(jnp.full((1, 1), a_ref[i_ref[l]], F32))
     load_f.wait()
-    for l in range(lat):
-        own_f[l] = f_in[:, l, :]
+
+    def move(act, src, dst, src_t, dst_t, i, sems, index, device):
+        w = pl.ds(0, full[i])
+        if full[i]:
+            act(src.at[:, w], dst.at[:, w], sems, index + (i,), device)
+        if i == final and rest:
+            act(src_t, dst_t, sems, index + (i + 1,), device)
+
+    def take(src, dst, sems, index, device):
+        got(dst, sems, index, device)
+
+    def value_of(ref, ref_t, i):
+        main = ref[:, : full[i]]
+        if i < final or not rest:
+            return main
+        return jnp.concatenate([main, unpack(ref_t[...], rest)], axis=1)
 
     def fill(ab, i):
         at, w = chunks[i]
-        send_f[ab, i, :, :w] = own_f[row_out[ab], :, at : at + w].astype(F32)
+        value = own_f[row_out[ab], :, at : at + w].astype(F32)
+        send_f[ab, i, :, : full[i]] = value[:, : full[i]]
+        if full[i] < w:
+            send_t[ab] = pack(value[:, full[i] :], rest)
 
     def send_fields(i):
-        w = chunks[i][1]
         for ab, to in ((0, to_x), (1, to_y)):
-            put(send_f.at[ab, i], recv_f.at[ab, i], sem_f, (ab, i), {"days": to})
+            move(put, send_f.at[ab, i], recv_f.at[ab, i], send_t.at[ab], recv_t.at[ab], i, sem_f, (ab,), {"days": to})
 
     early = len(chunks) - 1
     for i in range(len(chunks)):
+        at, w = chunks[i]
+        for l in range(lat):
+            own_f[l, :, at : at + w] = f_in[:, l, at : at + w]
         for ab in range(2):
             fill(ab, i)
         if i == 0:
@@ -167,8 +205,8 @@
         put(u_out.at[st, 0, 1 - c], r_one.at[st, 0], sem_one, (st, 0), core)
         if st > 0:
             for p, to in ((0, to_x), (1, to_y)):
-                put(u_out.at[st, 1 + p, c], r_one.at[st, 1 + 2 * p], sem_one, (st, 1 + 2 * p), {"days": to})
-                put(u_out.at[st, 1 + p, 1 - c], r_one.at[st, 2 + 2 * p], sem_one, (st, 2 + 2 * p), {"days": to, "space": other})
+                put(u_out.at[st, 1 + p, c, :, pl.ds(0, width)], r_one.at[st, 1 + 2 * p, :, pl.ds(0, width)], sem_one, (st, 1 + 2 * p), {"days": to})
+                put(u_out.at[st, 1 + p, 1 - c, :, pl.ds(0, width)], r_one.at[st, 2 + 2 * p, :, pl.ds(0, width)], sem_one, (st, 2 + 2 * p), {"days": to, "space": other})
         return rows
 
     def finish(st, hot, last):
@@ -181,8 +219,8 @@
             gram = (mine[:, base:width] + near[:, base:width], mine[:, width:] + near[:, width:])
             parts = []
             for p, to in ((0, to_x), (1, to_y)):
-                got(r_one.at[st, 1 + 2 * p], sem_one, (st, 1 + 2 * p), {"days": to})
-                got(r_one.at[st, 2 + 2 * p], sem_one, (st, 2 + 2 * p), {"days": to, "space": other})
+                got(r_one.at[st, 1 + 2 * p, :, pl.ds(0, width)], sem_one, (st, 1 + 2 * p), {"days": to})
+                got(r_one.at[st, 2 + 2 * p, :, pl.ds(0, width)], sem_one, (st, 2 + 2 * p), {"days": to, "space": other})
                 far = r_one[st, 1 + 2 * p, :, :width] + r_one[st, 2 + 2 * p, :, :width]
                 value = value + far
                 parts.append(gram[p] + far[:, base:])
@@ -269,12 +307,15 @@
         for i, (at, w) in enumerate(chunks):
             for ab, to, back in ((0, to_x, to_y), (1, to_y, to_x)):
                 if it == 0:
-                    got(recv_f.at[ab, i], sem_f, (ab, i), {"days": to})
-                    part_f[ab, :, at : at + w] = recv_f[ab, i, :, :w].astype(BF16)
+                    move(take, recv_f.at[ab, i], recv_f.at[ab, i], recv_t.at[ab], recv_t.at[ab], i, sem_f, (ab,), {"days": to})
+                    part_f[ab, :, at : at + w] = value_of(recv_f.at[ab, i], recv_t.at[ab], i).astype(BF16)
                 cover = join3(nn(patterns[0], own_f[row_of[ab], :, at : at + w])
                               + nn(patterns[1 + ab], part_f[ab, :, at : at + w]), modes)
                 c_send[it, ab, i, :, :w] = cover
-                put(c_send.at[it, ab, i], c_recv.at[it, ab, i], sem_c, (it, ab, i), {"days": back})
+                if full[i] < w:
+                    t_send[it, ab] = pack(cover[:, full[i] :], rest)
+                move(put, c_send.at[it, ab, i], c_recv.at[it, ab, i], t_send.at[it, ab], t_recv.at[it, ab], i,
+                     sem_c, (it, ab), {"days": back})
         raw = [None] * 3
         gram = [None] * 2
 
@@ -282,18 +323,20 @@
             sums[k] = term if sums[k] is None else sums[k] + term
 
         def spread(i):
-            w = chunks[i][1]
             for ab, to in ((0, to_x), (1, to_y)):
-                ref = c_all.at[row_of[ab], i]
-                put(ref, ref, sem_g, (ab, i), {"days": to})
+                ref, ref_t = c_all.at[row_of[ab], i], t_all.at[row_of[ab]]
+                move(put, ref, ref, ref_t, ref_t, i, sem_g, (ab,), {"days": to})
 
         for i, (at, w) in enumerate(chunks):
             for ab, back in ((0, to_y), (1, to_x)):
-                got(c_recv.at[it, ab, i], sem_c, (it, ab, i), {"days": back})
+                move(take, c_recv.at[it, ab, i], c_recv.at[it, ab, i], t_recv.at[it, ab], t_recv.at[it, ab], i,
+                     sem_c, (it, ab), {"days": back})
                 scale = s_ref[row_of[ab]]
-                cover = (c_send[it, ab, i, :, :w] + c_recv[it, ab, i, :, :w]) * (scale * (1.0 / n_days))
+                cover = (c_send[it, ab, i, :, :w] + value_of(c_recv.at[it, ab, i], t_recv.at[it, ab], i)) * (scale * (1.0 / n_days))
                 if last:
                     c_all[row_of[ab], i, :, :w] = cover
+                    if full[i] < w:
+                        t_all[row_of[ab]] = pack(cover[:, full[i] :], rest)
                 padded = jnp.concatenate([jnp.zeros((GRAM_AT, w), F32), cover], axis=0)
                 add(gram, ab, nt(cover, padded, precision=HIGH))
                 cover3 = split3(cover * scale)
@@ -302,7 +345,7 @@
             if last and i == 0:
                 spread(0)
         for b in range(3):
-            full = join3(raw[b], modes)
+            whole = join3(raw[b], modes)
             for half in range(2):
                 cut = slice(half * hm, (half + 1) * hm)
                 u_out[st, b, half, :, base:width] = gram[max(b - 1, 0)][cut]
@@ -310,11 +353,13 @@
                     u_out[st, b, half, :, width:] = gram[1][cut]
                 else:
                     u_out[st, b, half, :, width:] = jnp.zeros((hm, LANES), F32)
-                u_out[st, b, half, :, :dl] = full[cut]
+                u_out[st, b, half, :, :dl] = whole[cut]
         reduce(st, own_hot)
         if last:
             for i in range(1, len(chunks)):
                 spread(i)
+            for ab in range(2):
+                pltpu.make_async_copy(c_all.at[row_of[ab]], cover_hbm.at[row_of[ab]], sem_o.at[ab]).start()
         finish(st, own_hot, last)
         inv = inverse_factor(both(st, 0)[:, base:])
         if not last:
@@ -322,14 +367,20 @@
             mean = mean_of(st, last, per_day)
             patterns = [split3(nn(inv, center(both(st, b)[:, :dl], mean, hots[b]), precision=HIGH)) for b in range(3)]
         else:
-            for i, (at, w) in enumerate(chunks):
-                for ab, to in ((0, to_x), (1, to_y)):
-                    got(c_all.at[row_out[ab], i], sem_g, (ab, i), {"days": to})
-                for l in range(lat):
-                    eofs_ref[:, l, at : at + w] = nn(inv, c_all[l, i, :, :w], precision=HIGH)
+            inv_ref[...] = inv
+            for ab, to in ((0, to_x), (1, to_y)):
+                row = row_out[ab]
+                for i, (at, w) in enumerate(chunks):
+                    move(take, c_all.at[row, i], c_all.at[row, i], t_all.at[row], t_all.at[row], i, sem_g, (ab,), {"days": to})
+                if rest:
+                    c_all[row, final, :, full[final] : chunks[final][1]] = unpack(t_all[row], rest)
+                pltpu.make_async_copy(c_all.at[row], cover_hbm.at[row], sem_o.at[2 + ab]).start()
             forward(st, last)
             mean = mean_of(st, last, per_day)
             pcs_ref[...] = nn(inv, center(both(st, 0)[:, :dl], mean, own_hot), precision=HIGH)
+    for k in range(2 * 2):
+        row = (row_of + row_out)[k]
+        pltpu.make_async_copy(c_all.at[row], cover_hbm.at[row], sem_o.at[k]).wait()
     for d in started:
         d.wait_send()
 
@@ -348,18 +399,25 @@
         n = -(-lon // CHUNK)
         stages = ITERS + 1
         v, dma = pltpu.VMEM, pltpu.SemaphoreType.DMA
-        eofs, pcs = pl.pallas_call(
+        rest = lon % LANES
+        if rest and (LANES % rest or modes * rest % (8 * LANES) or dl * rest % (8 * LANES)):
+            raise ValueError("unsupported sizes")
+        spare = max(rest, 8)
+        cover, inv, pcs = pl.pallas_call(
             functools.partial(kernel, nd, ns),
-            out_shape=(jax.ShapeDtypeStruct((modes, lat, lon), F32), jax.ShapeDtypeStruct((modes, dl), F32)),
+            out_shape=(jax.ShapeDtypeStruct((lat, n, modes, CHUNK), F32), jax.ShapeDtypeStruct((modes, modes), F32),
+                       jax.ShapeDtypeStruct((modes, dl), F32)),
             in_specs=[pl.BlockSpec(memory_space=pl.ANY)] * 2 + [pl.BlockSpec(memory_space=pltpu.SMEM)] * 2
             + [pl.BlockSpec(memory_space=v)],
-            out_specs=(pl.BlockSpec(memory_space=v),) * 2,
+            out_specs=(pl.BlockSpec(memory_space=pl.ANY),) + (pl.BlockSpec(memory_space=v),) * 2,
             scratch_shapes=[
                 v((dl, lat, lon), BF16),
                 v((modes, lat, lon), BF16),
                 v((lat, dl, lon), BF16),
                 v((2, n, dl, CHUNK), F32),
                 v((2, n, dl, CHUNK), F32),
+                v((2, dl * spare // LANES, LANES), F32),
+                v((2, dl * spare // LANES, LANES), F32),
                 v((2, dl, lon), BF16),
                 v((lat, 1, 1), F32),
                 v((stages, 3, 2, hm, width + LANES), F32),
@@ -371,12 +429,25 @@
                 v((ITERS, 2, n, modes, CHUNK), F32),
                 v((ITERS, 2, n, modes, CHUNK), F32),
                 v((lat, n, modes, CHUNK), F32),
-                dma((2,)), dma((2, 2, n)), dma((2, stages, 5)), dma((2, stages, nz - 1)),
-                dma((2, stages, 4)), dma((2, stages, 3)), dma((2, ITERS, 2, n)), dma((2, 2, n)),
+                v((ITERS, 2, modes * spare // LANES, LANES), F32),
+                v((ITERS, 2, modes * spare // LANES, LANES), F32),
+                v((lat, modes * spare // LANES, LANES), F32),
+                dma((2,)), dma((2, 2, n + 1)), dma((2, stages, 5)), dma((2, stages, nz - 1)),
+                dma((2, stages, 4)), dma((2, stages, 3)), dma((2, ITERS, 2, n + 1)), dma((2, 2, n + 1)),
+                dma((4,)),
             ],
             compiler_params=pltpu.CompilerParams(
                 collective_id=0, has_side_effects=True, vmem_limit_bytes=60 * 1024 * 1024),
         )(fields, basis, row_index, area_table, month_label[None, :])
+        eofs, pcs = pl.pallas_call(
+            last_kernel,
+            grid=(n,),
+            out_shape=(jax.ShapeDtypeStruct((modes, lat, lon), F32), jax.ShapeDtypeStruct((modes, dl), F32)),
+            in_specs=[pl.BlockSpec((modes, modes), lambda i: (0, 0)),
+                      pl.BlockSpec((lat, 1, modes, CHUNK), lambda i: (0, i, 0, 0)),
+                      pl.BlockSpec((modes, dl), lambda i: (0, 0))],
+            out_specs=(pl.BlockSpec((modes, lat, CHUNK), lambda i: (0, 0, i)), pl.BlockSpec((modes, dl), lambda i: (0, 0))),
+        )(inv, cover, pcs)
         return eofs, pcs.T
 
     placed = (P("days", "space", None), P("days"), P("space"), P(), P(None, "space", None))

time: 90.5 us -> 85.2 us (0.941)
  local copies, waits for them, and re-layouts: 3.32 us -> 0 us
  Pallas kernels: 86.3 us -> 84.3 us
    pallas_call x1, Pallas kernels: 86.3 us -> 79.8 us  [local(): pl.pallas_call(functools.partial(kernel, nd, ns), out_shape=(jax.ShapeDty...]
    pallas_call x0 -> x1, Pallas kernels: none -> 4.51 us  [local(): pl.pallas_call(last_kernel, grid=(n,), out_shape=(jax.ShapeDtypeStruct((m...]
    unnamed x4 -> x0, local copies, waits for them, and re-layouts: 3.32 us -> none
where the time goes in v2:
time: 85.2 us; the launch traced here: 84.9 us
  Pallas kernels  84.3 us (99%)
    pallas_call x1, Pallas kernels, local(): pl.pallas_call(functools.partial(kernel, nd, ns), out_shape=(jax.ShapeDty...  79.8 us
    pallas_call x1, Pallas kernels, local(): pl.pallas_call(last_kernel, grid=(n,), out_shape=(jax.ShapeDtypeStruct((m...  4.51 us

profile of v2, /device:TPU:0, one launch (start us, length us, event | category | flops | bytes accessed | tf_op | source)
XLA Modules:
  0.0 84.9 jit_solution(5538194387841314689)
XLA Ops:
  0.6 79.8 %shard_map.68 = (f32[4,4,64,384]{3,2,1,0:T(8,128)}, f32[64,64]{1,0:T(8,128)}, f32[64,160]{1,0:T(8,128)}) custom-call(bf16[160,4,1440]{2,1,0:T(4,128)(2,1)} %f_hbm.1, bf16[64,4,1440]{2,1,0:T(4,128)(2,1)} %b_hbm.1, s32[4]{0:T(128)} %i_ref.1, f32[32]{0:T(128)} %a_ref.1, s32[1,160]{1,0:T(1,128)} %bitcast.2), custom_call_target="tpu_custom_call" | custom-call | tf_op jit(solution)/shard_map/pallas_call | solution.py:406
  80.4 4.5 %shard_map.69 = (f32[64,4,1440]{2,1,0:T(4,128)}, f32[64,160]{1,0:T(8,128)}) custom-call(f32[64,64]{1,0:T(8,128)} %get-tuple-element.7.inv_ref, f32[4,4,64,384]{3,2,1,0:T(8,128)} %get-tuple-element.8.cover_ref, f32[64,160]{1,0:T(8,128)} %get-tuple-element.9.pcs_ref), custom_call_target="tpu_custom_call" | custom-call | tf_op jit(solution)/shard_map/pallas_call | solution.py:442

commit v3 on v2

--- a/solution.py
+++ b/solution.py
@@ -10,7 +10,6 @@
 ITERS = 2
 MONTHS = 12
 MESH = pl.DeviceIdType.MESH
-HIGH = lax.Precision.HIGHEST
 F32 = jnp.float32
 BF16 = jnp.bfloat16
 LANES = 128
@@ -28,16 +27,28 @@
     return lax.dot_general(a, b, (((1,), (0,)), ((), ())), preferred_element_type=F32, **kw)
 
 
-def split3(x):
+def halves(x):
     high = x.astype(BF16)
-    rest = x - high.astype(F32)
-    mid = rest.astype(BF16)
-    low = (rest - mid.astype(F32)).astype(BF16)
-    return jnp.concatenate([high, mid, low], axis=0)
-
-
-def join3(x, n):
-    return x[:n] + (x[n : 2 * n] + x[2 * n :])
+    return high, (x - high.astype(F32)).astype(BF16)
+
+
+def split(x):
+    return jnp.concatenate(halves(x), axis=0)
+
+
+def join(x):
+    n = x.shape[0] // 2
+    return x[:n] + x[n:]
+
+
+def factor(inv):
+    high, low = halves(inv)
+    return jnp.concatenate([high, low, high, low], axis=1)
+
+
+def apply(inv4, x):
+    high, low = halves(x)
+    return nn(inv4, jnp.concatenate([high, high, low, low], axis=0))
 
 
 def tree(terms):
@@ -80,18 +91,18 @@
 
 
 def last_kernel(inv_ref, cover_ref, pcs_ref, eofs_ref, out_ref):
-    inv = inv_ref[...]
+    inv4 = factor(inv_ref[...])
     for l in range(eofs_ref.shape[1]):
-        eofs_ref[:, l, :] = nn(inv, cover_ref[l, 0], precision=HIGH)
+        eofs_ref[:, l, :] = apply(inv4, cover_ref[l, 0])
     out_ref[...] = pcs_ref[...]
 
 
-def kernel(nd, ns, f_hbm, b_hbm, i_ref, a_ref, l_ref, cover_hbm, inv_ref, pcs_ref,
-           f_in, b_in, own_f, send_f, recv_f, send_t, recv_t, part_f, s_ref,
+def kernel(nd, ns, f_hbm, b_hbm, i_ref, a_ref, l_ref, cover_hbm, inv_hbm, pcs_hbm,
+           inv_ref, pcs_ref, f_in, wide_f, b_in, own_f, send_f, recv_f, send_t, recv_t, part_f, s_ref,
            u_out, r_one, v_out, r_two, blk, tl, c_send, c_recv, c_all, t_send, t_recv, t_all,
            sem_l, sem_f, sem_one, sem_two, sem_b, sem_fw, sem_c, sem_g, sem_o):
     dl, lat, lon = f_in.shape
-    modes = inv_ref.shape[0]
+    modes = b_in.shape[0]
     hm = modes // 2
     base = dl // LANES * LANES
     tail = dl - base
@@ -179,8 +190,9 @@
     early = len(chunks) - 1
     for i in range(len(chunks)):
         at, w = chunks[i]
+        wide_f[i % 2, :, :, :w] = f_in[:, :, at : at + w].astype(F32)
         for l in range(lat):
-            own_f[l, :, at : at + w] = f_in[:, l, at : at + w]
+            own_f[l, :, at : at + w] = wide_f[i % 2, :, l, :w].astype(BF16)
         for ab in range(2):
             fill(ab, i)
         if i == 0:
@@ -234,7 +246,7 @@
         for k in range(1, nz):
             got(r_two.at[st, k - 1], sem_two, (st, k - 1), {"space": z_peer(k)})
         value = tree([v_out[st]] + [r_two[st, k - 1] for k in range(1, nz)])
-        month = join3(nt(split3(value[:, :dl]), hot), hm)
+        month = join(nt(split(value[:, :dl]), hot))
         blk[st, 0, c, :hm, :base] = value[:, :base]
         blk[st, 0, c, :hm, base:] = value[:, base:] + month
         if st == 0:
@@ -248,7 +260,10 @@
             if p < 2 and not last:
                 put(mine, blk.at[st, 1 + p, c, pl.ds(0, rows)], sem_b, (st, p), {"days": to})
             else:
-                put(blk.at[st, 0, c, pl.ds(0, rows), pl.ds(base, LANES)], tl.at[st, p, c, pl.ds(0, rows)], sem_b, (st, p), {"days": to})
+                tile = blk.at[st, 0, c, pl.ds(0, rows), pl.ds(base, LANES)]
+                put(tile, tl.at[st, p, c, pl.ds(0, rows)], sem_b, (st, p), {"days": to})
+                if last:
+                    put(tile, tl.at[st, p, c, pl.ds(0, rows)], sem_fw, (st, p), {"days": to, "space": other})
         theirs = blk.at[st, 0, 1 - c, pl.ds(0, rows)]
         got(theirs, sem_b, (st, 3), core)
 
@@ -262,9 +277,11 @@
         for p, to in ((0, to_x), (1, to_y), (2, to_d)):
             ref = landed(st, last, p, c)
             got(ref, sem_b, (st, p), {"days": to})
-            put(ref, ref, sem_fw, (st, p), core)
-        for p in range(3):
-            got(landed(st, last, p, 1 - c), sem_fw, (st, p), core)
+            if not last:
+                put(ref, ref, sem_fw, (st, p), core)
+        for p, to in ((0, to_x), (1, to_y), (2, to_d)):
+            device = {"days": to, "space": other} if last else core
+            got(landed(st, last, p, 1 - c), sem_fw, (st, p), device)
 
     def both(st, b):
         return jnp.concatenate([blk[st, b, 0, :hm], blk[st, b, 1, :hm]], axis=0)
@@ -281,10 +298,10 @@
     def mean_of(st, last, scale):
         sums = tree(tiles(st, last))
         inside = (lane >= tail) & (lane < tail + MONTHS)
-        return split3(jnp.where(inside, sums * scale, 0.0))
+        return split(jnp.where(inside, sums * scale, 0.0))
 
     def center(value, mean, hot):
-        return value - join3(nn(mean, hot), modes)
+        return value - join(nn(mean, hot))
 
     own_hot = hot_of(l_ref[...].astype(F32))
     for half in range(2):
@@ -299,7 +316,7 @@
     counts = tree([blk[0, b, 0, hm : hm + 1, base:] for b in range(3)] + [tl[0, 2, 0, hm : hm + 1]])
     per_day = 1.0 / jnp.maximum(counts, 1.0)
     mean = mean_of(0, False, per_day)
-    patterns = [split3(center(both(0, b)[:, :dl], mean, hots[b])) for b in range(3)]
+    patterns = [split(center(both(0, b)[:, :dl], mean, hots[b])) for b in range(3)]
 
     for it in range(ITERS):
         st = it + 1
@@ -309,14 +326,14 @@
                 if it == 0:
                     move(take, recv_f.at[ab, i], recv_f.at[ab, i], recv_t.at[ab], recv_t.at[ab], i, sem_f, (ab,), {"days": to})
                     part_f[ab, :, at : at + w] = value_of(recv_f.at[ab, i], recv_t.at[ab], i).astype(BF16)
-                cover = join3(nn(patterns[0], own_f[row_of[ab], :, at : at + w])
-                              + nn(patterns[1 + ab], part_f[ab, :, at : at + w]), modes)
+                cover = join(nn(patterns[0], own_f[row_of[ab], :, at : at + w])
+                             + nn(patterns[1 + ab], part_f[ab, :, at : at + w]))
                 c_send[it, ab, i, :, :w] = cover
                 if full[i] < w:
                     t_send[it, ab] = pack(cover[:, full[i] :], rest)
                 move(put, c_send.at[it, ab, i], c_recv.at[it, ab, i], t_send.at[it, ab], t_recv.at[it, ab], i,
                      sem_c, (it, ab), {"days": back})
-        raw = [None] * 3
+        raw = [None] * 4
         gram = [None] * 2
 
         def add(sums, k, term):
@@ -331,21 +348,23 @@
             for ab, back in ((0, to_y), (1, to_x)):
                 move(take, c_recv.at[it, ab, i], c_recv.at[it, ab, i], t_recv.at[it, ab], t_recv.at[it, ab], i,
                      sem_c, (it, ab), {"days": back})
-                scale = s_ref[row_of[ab]]
-                cover = (c_send[it, ab, i, :, :w] + value_of(c_recv.at[it, ab, i], t_recv.at[it, ab], i)) * (scale * (1.0 / n_days))
+                cover = (c_send[it, ab, i, :, :w] + value_of(c_recv.at[it, ab, i], t_recv.at[it, ab], i)) * (s_ref[row_of[ab]] * (1.0 / n_days))
                 if last:
                     c_all[row_of[ab], i, :, :w] = cover
                     if full[i] < w:
                         t_all[row_of[ab]] = pack(cover[:, full[i] :], rest)
-                padded = jnp.concatenate([jnp.zeros((GRAM_AT, w), F32), cover], axis=0)
-                add(gram, ab, nt(cover, padded, precision=HIGH))
-                cover3 = split3(cover * scale)
-                add(raw, 0, nt(cover3, own_f[row_of[ab], :, at : at + w]))
-                add(raw, 1 + ab, nt(cover3, part_f[ab, :, at : at + w]))
+                cover2 = split(cover)
+                add(gram, ab, nt(cover2, cover2))
+                add(raw, 2 * ab, nt(cover2, own_f[row_of[ab], :, at : at + w]))
+                add(raw, 2 * ab + 1, nt(cover2, part_f[ab, :, at : at + w]))
             if last and i == 0:
                 spread(0)
+        gram = [join(g) for g in gram]
+        gram = [jnp.where(lane < GRAM_AT, 0.0, g + pltpu.roll(g, GRAM_AT, 1)) for g in gram]
+        raw = [join(raw[k]) * s_ref[row_of[k // 2]] for k in range(4)]
+        raw = (raw[0] + raw[2], raw[1], raw[3])
         for b in range(3):
-            whole = join3(raw[b], modes)
+            whole = raw[b]
             for half in range(2):
                 cut = slice(half * hm, (half + 1) * hm)
                 u_out[st, b, half, :, base:width] = gram[max(b - 1, 0)][cut]
@@ -362,12 +381,14 @@
                 pltpu.make_async_copy(c_all.at[row_of[ab]], cover_hbm.at[row_of[ab]], sem_o.at[ab]).start()
         finish(st, own_hot, last)
         inv = inverse_factor(both(st, 0)[:, base:])
+        inv4 = factor(inv)
         if not last:
             forward(st, last)
             mean = mean_of(st, last, per_day)
-            patterns = [split3(nn(inv, center(both(st, b)[:, :dl], mean, hots[b]), precision=HIGH)) for b in range(3)]
+            patterns = [split(apply(inv4, center(both(st, b)[:, :dl], mean, hots[b]))) for b in range(3)]
         else:
             inv_ref[...] = inv
+            pltpu.make_async_copy(inv_ref, inv_hbm, sem_o.at[4]).start()
             for ab, to in ((0, to_x), (1, to_y)):
                 row = row_out[ab]
                 for i, (at, w) in enumerate(chunks):
@@ -377,12 +398,15 @@
                 pltpu.make_async_copy(c_all.at[row], cover_hbm.at[row], sem_o.at[2 + ab]).start()
             forward(st, last)
             mean = mean_of(st, last, per_day)
-            pcs_ref[...] = nn(inv, center(both(st, 0)[:, :dl], mean, own_hot), precision=HIGH)
+            pcs_ref[...] = apply(inv4, center(both(st, 0)[:, :dl], mean, own_hot))
+            pltpu.make_async_copy(pcs_ref, pcs_hbm, sem_o.at[5]).start()
     for k in range(2 * 2):
         row = (row_of + row_out)[k]
         pltpu.make_async_copy(c_all.at[row], cover_hbm.at[row], sem_o.at[k]).wait()
     for d in started:
         d.wait_send()
+    pltpu.make_async_copy(inv_ref, inv_hbm, sem_o.at[4]).wait()
+    pltpu.make_async_copy(pcs_ref, pcs_hbm, sem_o.at[5]).wait()
 
 
 def solution(mesh):
@@ -394,7 +418,7 @@
         hm, nz = modes // 2, ns // 2
         base = dl // LANES * LANES
         width = base + LANES
-        if nd != 4 or lat != nd or modes > GRAM_AT or dl - base + MONTHS > GRAM_AT or nz & (nz - 1):
+        if nd != 4 or lat != nd or modes != GRAM_AT or dl - base + MONTHS > GRAM_AT or nz & (nz - 1):
             raise ValueError("unsupported sizes")
         n = -(-lon // CHUNK)
         stages = ITERS + 1
@@ -409,9 +433,12 @@
                        jax.ShapeDtypeStruct((modes, dl), F32)),
             in_specs=[pl.BlockSpec(memory_space=pl.ANY)] * 2 + [pl.BlockSpec(memory_space=pltpu.SMEM)] * 2
             + [pl.BlockSpec(memory_space=v)],
-            out_specs=(pl.BlockSpec(memory_space=pl.ANY),) + (pl.BlockSpec(memory_space=v),) * 2,
+            out_specs=(pl.BlockSpec(memory_space=pl.ANY),) * 3,
             scratch_shapes=[
+                v((modes, modes), F32),
+                v((modes, dl), F32),
                 v((dl, lat, lon), BF16),
+                v((2, dl, lat, CHUNK), F32),
                 v((modes, lat, lon), BF16),
                 v((lat, dl, lon), BF16),
                 v((2, n, dl, CHUNK), F32),
@@ -434,7 +461,7 @@
                 v((lat, modes * spare // LANES, LANES), F32),
                 dma((2,)), dma((2, 2, n + 1)), dma((2, stages, 5)), dma((2, stages, nz - 1)),
                 dma((2, stages, 4)), dma((2, stages, 3)), dma((2, ITERS, 2, n + 1)), dma((2, 2, n + 1)),
-                dma((4,)),
+                dma((6,)),
             ],
             compiler_params=pltpu.CompilerParams(
                 collective_id=0, has_side_effects=True, vmem_limit_bytes=60 * 1024 * 1024),

time: 85.2 us -> 82.7 us (0.971)
  Pallas kernels: 84.3 us -> 81.8 us
    pallas_call x1, Pallas kernels: 79.8 us -> 77.6 us  [local(): pl.pallas_call(functools.partial(kernel, nd, ns), out_shape=(jax.ShapeDty...]
where the time goes in v3:
time: 82.7 us; the launch traced here: 82.4 us
  Pallas kernels  81.8 us (99%)
    pallas_call x1, Pallas kernels, local(): pl.pallas_call(functools.partial(kernel, nd, ns), out_shape=(jax.ShapeDty...  77.6 us
    pallas_call x1, Pallas kernels, local(): pl.pallas_call(last_kernel, grid=(n,), out_shape=(jax.ShapeDtypeStruct((m...  4.16 us

profile of v3, /device:TPU:0, one launch (start us, length us, event | category | flops | bytes accessed | tf_op | source)
XLA Modules:
  0.0 82.4 jit_solution(6074637451738346116)
XLA Ops:
  0.6 77.6 %shard_map.68 = (f32[4,4,64,384]{3,2,1,0:T(8,128)}, f32[64,64]{1,0:T(8,128)}, f32[64,160]{1,0:T(8,128)}) custom-call(bf16[160,4,1440]{2,1,0:T(4,128)(2,1)} %f_hbm.1, bf16[64,4,1440]{2,1,0:T(4,128)(2,1)} %b_hbm.1, s32[4]{0:T(128)} %i_ref.1, f32[32]{0:T(128)} %a_ref.1, s32[1,160]{1,0:T(1,128)} %bitcast.2), custom_call_target="tpu_custom_call" | custom-call | tf_op jit(solution)/shard_map/pallas_call | solution.py:430
  78.3 4.2 %shard_map.69 = (f32[64,4,1440]{2,1,0:T(4,128)}, f32[64,160]{1,0:T(8,128)}) custom-call(f32[64,64]{1,0:T(8,128)} %get-tuple-element.7.inv_ref, f32[4,4,64,384]{3,2,1,0:T(8,128)} %get-tuple-element.8.cover_ref, f32[64,160]{1,0:T(8,128)} %get-tuple-element.9.pcs_ref), custom_call_target="tpu_custom_call" | custom-call | tf_op jit(solution)/shard_map/pallas_call | solution.py:469

commit v4 on v3

--- a/solution.py
+++ b/solution.py
@@ -13,7 +13,9 @@
 F32 = jnp.float32
 BF16 = jnp.bfloat16
 LANES = 128
-CHUNK = 3 * LANES
+STEP = 4 * LANES
+SIZES = (2, 3, 3, 2)
+EARLY = 3
 EXTRA = 8
 GRAM_AT = LANES // 2
 BLOCK = 4
@@ -27,6 +29,10 @@
     return lax.dot_general(a, b, (((1,), (0,)), ((), ())), preferred_element_type=F32, **kw)
 
 
+def up(value, step):
+    return -(-value // step) * step
+
+
 def halves(x):
     high = x.astype(BF16)
     return high, (x - high.astype(F32)).astype(BF16)
@@ -49,6 +55,20 @@
 def apply(inv4, x):
     high, low = halves(x)
     return nn(inv4, jnp.concatenate([high, high, low, low], axis=0))
+
+
+def cuts(lon):
+    tiles = -(-lon // LANES)
+    sizes = []
+    for size in SIZES + (2,) * tiles:
+        size = min(size, tiles - sum(sizes))
+        if size:
+            sizes.append(size)
+    out, at = [], 0
+    for size in sizes:
+        out.append((at, min(size * LANES, lon - at)))
+        at += size * LANES
+    return out
 
 
 def tree(terms):
@@ -93,7 +113,7 @@
 def last_kernel(inv_ref, cover_ref, pcs_ref, eofs_ref, out_ref):
     inv4 = factor(inv_ref[...])
     for l in range(eofs_ref.shape[1]):
-        eofs_ref[:, l, :] = apply(inv4, cover_ref[l, 0])
+        eofs_ref[:, l, :] = apply(inv4, cover_ref[l])
     out_ref[...] = pcs_ref[...]
 
 
@@ -108,7 +128,7 @@
     tail = dl - base
     width = base + LANES
     nz = ns // 2
-    chunks = [(at, min(CHUNK, lon - at)) for at in range(0, lon, CHUNK)]
+    chunks = cuts(lon)
     n_days = nd * dl
     rest = lon % LANES
     final = len(chunks) - 1
@@ -161,7 +181,7 @@
     load_f.wait()
 
     def move(act, src, dst, src_t, dst_t, i, sems, index, device):
-        w = pl.ds(0, full[i])
+        w = pl.ds(chunks[i][0], full[i])
         if full[i]:
             act(src.at[:, w], dst.at[:, w], sems, index + (i,), device)
         if i == final and rest:
@@ -171,40 +191,31 @@
         got(dst, sems, index, device)
 
     def value_of(ref, ref_t, i):
-        main = ref[:, : full[i]]
+        main = ref[:, chunks[i][0] : chunks[i][0] + full[i]]
         if i < final or not rest:
             return main
         return jnp.concatenate([main, unpack(ref_t[...], rest)], axis=1)
 
-    def fill(ab, i):
-        at, w = chunks[i]
-        value = own_f[row_out[ab], :, at : at + w].astype(F32)
-        send_f[ab, i, :, : full[i]] = value[:, : full[i]]
-        if full[i] < w:
-            send_t[ab] = pack(value[:, full[i] :], rest)
-
     def send_fields(i):
         for ab, to in ((0, to_x), (1, to_y)):
-            move(put, send_f.at[ab, i], recv_f.at[ab, i], send_t.at[ab], recv_t.at[ab], i, sem_f, (ab,), {"days": to})
-
-    early = len(chunks) - 1
+            move(put, send_f.at[row_out[ab]], recv_f.at[ab], send_t.at[row_out[ab]], recv_t.at[ab], i, sem_f, (ab,), {"days": to})
+
+    early = min(EARLY, len(chunks))
     for i in range(len(chunks)):
         at, w = chunks[i]
-        wide_f[i % 2, :, :, :w] = f_in[:, :, at : at + w].astype(F32)
+        wide_f[:, :, at : at + w] = f_in[:, :, at : at + w].astype(F32)
         for l in range(lat):
-            own_f[l, :, at : at + w] = wide_f[i % 2, :, l, :w].astype(BF16)
-        for ab in range(2):
-            fill(ab, i)
+            value = wide_f[:, l, at : at + w]
+            send_f[l, :, at : at + full[i]] = value[:, : full[i]]
+            if full[i] < w:
+                send_t[l] = pack(value[:, full[i] :], rest)
+            own_f[l, :, at : at + w] = value.astype(BF16)
         if i == 0:
             pl.semaphore_wait(barrier, len(friends))
         if i < early:
             send_fields(i)
-
     load_b.wait()
-    total = None
-    for l in range(lat):
-        term = nt(b_in[:, l, :], own_f[l]) * s_ref[l]
-        total = term if total is None else total + term
+    total = tree([nt(b_in[:, l, :], own_f[l]) * s_ref[l] for l in range(lat)])
 
     lane = lax.broadcasted_iota(jnp.int32, (1, LANES), 1)
 
@@ -324,14 +335,14 @@
         for i, (at, w) in enumerate(chunks):
             for ab, to, back in ((0, to_x, to_y), (1, to_y, to_x)):
                 if it == 0:
-                    move(take, recv_f.at[ab, i], recv_f.at[ab, i], recv_t.at[ab], recv_t.at[ab], i, sem_f, (ab,), {"days": to})
-                    part_f[ab, :, at : at + w] = value_of(recv_f.at[ab, i], recv_t.at[ab], i).astype(BF16)
+                    move(take, recv_f.at[ab], recv_f.at[ab], recv_t.at[ab], recv_t.at[ab], i, sem_f, (ab,), {"days": to})
+                    part_f[ab, :, at : at + w] = value_of(recv_f.at[ab], recv_t.at[ab], i).astype(BF16)
                 cover = join(nn(patterns[0], own_f[row_of[ab], :, at : at + w])
                              + nn(patterns[1 + ab], part_f[ab, :, at : at + w]))
-                c_send[it, ab, i, :, :w] = cover
+                c_send[it, ab, :, at : at + w] = cover
                 if full[i] < w:
                     t_send[it, ab] = pack(cover[:, full[i] :], rest)
-                move(put, c_send.at[it, ab, i], c_recv.at[it, ab, i], t_send.at[it, ab], t_recv.at[it, ab], i,
+                move(put, c_send.at[it, ab], c_recv.at[it, ab], t_send.at[it, ab], t_recv.at[it, ab], i,
                      sem_c, (it, ab), {"days": back})
         raw = [None] * 4
         gram = [None] * 2
@@ -341,16 +352,16 @@
 
         def spread(i):
             for ab, to in ((0, to_x), (1, to_y)):
-                ref, ref_t = c_all.at[row_of[ab], i], t_all.at[row_of[ab]]
+                ref, ref_t = c_all.at[row_of[ab]], t_all.at[row_of[ab]]
                 move(put, ref, ref, ref_t, ref_t, i, sem_g, (ab,), {"days": to})
 
         for i, (at, w) in enumerate(chunks):
             for ab, back in ((0, to_y), (1, to_x)):
-                move(take, c_recv.at[it, ab, i], c_recv.at[it, ab, i], t_recv.at[it, ab], t_recv.at[it, ab], i,
+                move(take, c_recv.at[it, ab], c_recv.at[it, ab], t_recv.at[it, ab], t_recv.at[it, ab], i,
                      sem_c, (it, ab), {"days": back})
-                cover = (c_send[it, ab, i, :, :w] + value_of(c_recv.at[it, ab, i], t_recv.at[it, ab], i)) * (s_ref[row_of[ab]] * (1.0 / n_days))
+                cover = (c_send[it, ab, :, at : at + w] + value_of(c_recv.at[it, ab], t_recv.at[it, ab], i)) * (s_ref[row_of[ab]] * (1.0 / n_days))
                 if last:
-                    c_all[row_of[ab], i, :, :w] = cover
+                    c_all[row_of[ab], :, at : at + w] = cover
                     if full[i] < w:
                         t_all[row_of[ab]] = pack(cover[:, full[i] :], rest)
                 cover2 = split(cover)
@@ -392,9 +403,9 @@
             for ab, to in ((0, to_x), (1, to_y)):
                 row = row_out[ab]
                 for i, (at, w) in enumerate(chunks):
-                    move(take, c_all.at[row, i], c_all.at[row, i], t_all.at[row], t_all.at[row], i, sem_g, (ab,), {"days": to})
+                    move(take, c_all.at[row], c_all.at[row], t_all.at[row], t_all.at[row], i, sem_g, (ab,), {"days": to})
                 if rest:
-                    c_all[row, final, :, full[final] : chunks[final][1]] = unpack(t_all[row], rest)
+                    c_all[row, :, lon - rest : lon] = unpack(t_all[row], rest)
                 pltpu.make_async_copy(c_all.at[row], cover_hbm.at[row], sem_o.at[2 + ab]).start()
             forward(st, last)
             mean = mean_of(st, last, per_day)
@@ -420,7 +431,7 @@
         width = base + LANES
         if nd != 4 or lat != nd or modes != GRAM_AT or dl - base + MONTHS > GRAM_AT or nz & (nz - 1):
             raise ValueError("unsupported sizes")
-        n = -(-lon // CHUNK)
+        n, span = len(cuts(lon)), up(lon, LANES)
         stages = ITERS + 1
         v, dma = pltpu.VMEM, pltpu.SemaphoreType.DMA
         rest = lon % LANES
@@ -429,7 +440,7 @@
         spare = max(rest, 8)
         cover, inv, pcs = pl.pallas_call(
             functools.partial(kernel, nd, ns),
-            out_shape=(jax.ShapeDtypeStruct((lat, n, modes, CHUNK), F32), jax.ShapeDtypeStruct((modes, modes), F32),
+            out_shape=(jax.ShapeDtypeStruct((lat, modes, span), F32), jax.ShapeDtypeStruct((modes, modes), F32),
                        jax.ShapeDtypeStruct((modes, dl), F32)),
             in_specs=[pl.BlockSpec(memory_space=pl.ANY)] * 2 + [pl.BlockSpec(memory_space=pltpu.SMEM)] * 2
             + [pl.BlockSpec(memory_space=v)],
@@ -438,12 +449,12 @@
                 v((modes, modes), F32),
                 v((modes, dl), F32),
                 v((dl, lat, lon), BF16),
-                v((2, dl, lat, CHUNK), F32),
+                v((dl, lat, span), F32),
                 v((modes, lat, lon), BF16),
                 v((lat, dl, lon), BF16),
-                v((2, n, dl, CHUNK), F32),
-                v((2, n, dl, CHUNK), F32),
-                v((2, dl * spare // LANES, LANES), F32),
+                v((lat, dl, span), F32),
+                v((2, dl, span), F32),
+                v((lat, dl * spare // LANES, LANES), F32),
                 v((2, dl * spare // LANES, LANES), F32),
                 v((2, dl, lon), BF16),
                 v((lat, 1, 1), F32),
@@ -453,9 +464,9 @@
                 v((stages, nz - 1, hm, width), F32),
                 v((stages, 3, 2, hm + EXTRA, width), F32),
                 v((stages, 3, 2, hm + EXTRA, LANES), F32),
-                v((ITERS, 2, n, modes, CHUNK), F32),
-                v((ITERS, 2, n, modes, CHUNK), F32),
-                v((lat, n, modes, CHUNK), F32),
+                v((ITERS, 2, modes, span), F32),
+                v((ITERS, 2, modes, span), F32),
+                v((lat, modes, span), F32),
                 v((ITERS, 2, modes * spare // LANES, LANES), F32),
                 v((ITERS, 2, modes * spare // LANES, LANES), F32),
                 v((lat, modes * spare // LANES, LANES), F32),
@@ -468,12 +479,12 @@
         )(fields, basis, row_index, area_table, month_label[None, :])
         eofs, pcs = pl.pallas_call(
             last_kernel,
-            grid=(n,),
+            grid=(-(-span // STEP),),
             out_shape=(jax.ShapeDtypeStruct((modes, lat, lon), F32), jax.ShapeDtypeStruct((modes, dl), F32)),
             in_specs=[pl.BlockSpec((modes, modes), lambda i: (0, 0)),
-                      pl.BlockSpec((lat, 1, modes, CHUNK), lambda i: (0, i, 0, 0)),
+                      pl.BlockSpec((lat, modes, STEP), lambda i: (0, 0, i)),
                       pl.BlockSpec((modes, dl), lambda i: (0, 0))],
-            out_specs=(pl.BlockSpec((modes, lat, CHUNK), lambda i: (0, 0, i)), pl.BlockSpec((modes, dl), lambda i: (0, 0))),
+            out_specs=(pl.BlockSpec((modes, lat, STEP), lambda i: (0, 0, i)), pl.BlockSpec((modes, dl), lambda i: (0, 0))),
         )(inv, cover, pcs)
         return eofs, pcs.T
 

time: 82.7 us -> 81.8 us (0.989)
  no operation moved by 1% of the time
where the time goes in v4:
time: 81.8 us; the launch traced here: 81.6 us
  Pallas kernels  81 us (99%)
    pallas_call x1, Pallas kernels, local(): pl.pallas_call(functools.partial(kernel, nd, ns), out_shape=(jax.ShapeDty...  77.2 us
    pallas_call x1, Pallas kernels, local(): pl.pallas_call(last_kernel, grid=(-(-span // STEP),), out_shape=(jax.Shap...  3.81 us

profile of v4, /device:TPU:0, one launch (start us, length us, event | category | flops | bytes accessed | tf_op | source)
XLA Modules:
  0.0 81.6 jit_solution(10303086714889533968)
XLA Ops:
  0.6 77.2 %shard_map.68 = (f32[4,64,1536]{2,1,0:T(8,128)}, f32[64,64]{1,0:T(8,128)}, f32[64,160]{1,0:T(8,128)}) custom-call(bf16[160,4,1440]{2,1,0:T(4,128)(2,1)} %f_hbm.1, bf16[64,4,1440]{2,1,0:T(4,128)(2,1)} %b_hbm.1, s32[4]{0:T(128)} %i_ref.1, f32[32]{0:T(128)} %a_ref.1, s32[1,160]{1,0:T(1,128)} %bitcast.2), custom_call_target="tpu_custom_call" | custom-call | tf_op jit(solution)/shard_map/pallas_call | solution.py:441
  77.8 3.8 %shard_map.69 = (f32[64,4,1440]{2,1,0:T(4,128)}, f32[64,160]{1,0:T(8,128)}) custom-call(f32[64,64]{1,0:T(8,128)} %get-tuple-element.7.inv_ref, f32[4,64,1536]{2,1,0:T(8,128)} %get-tuple-element.8.cover_ref, f32[64,160]{1,0:T(8,128)} %get-tuple-element.9.pcs_ref), custom_call_target="tpu_custom_call" | custom-call | tf_op jit(solution)/shard_map/pallas_call | solution.py:480
